TPU v7x, 32 devices: a whole 2x2x4 slice. The times are simulated.
32 devices in a mesh: pts: 8 (over z, x), grp: 4 (over y, core).
Axes of the slice: x: 2, y: 2, z: 4, core: 2. Of those that a mesh axis runs over, the one named last changes fastest.
Arguments:
- embeddings: bfloat16 [131072, 1024], P(('pts', 'grp')), as said below
- best_start: float32 [131072], P(('pts', 'grp')), may hold values from 0 to 2
- bounds_start: float32 [131072], P(('pts', 'grp')), may hold values from 0 to 4
- proposals: int32 [8, 32], replicated, may hold values from 0 to 131071
Outputs:
- gain_table: float32 [8, 32], replicated
- coverage: float32 [8], replicated
- best_final: float32 [131072], P(('pts', 'grp'))
- bounds_final: float32 [131072], P(('pts', 'grp'))
Inputs may be any that keep to these rules, and one draw needn't show every extreme that they name: Rows are real valued embeddings of varying norm.
All inputs are finite; a program needn't handle non-finite values.
Results may differ from a plain program's by a relative error of at most 0.0003.
Values may be sent and summed in bfloat16 or wider, within the bound.
A program may use at most 64 MiB of HBM per device.

v0:
```python
import jax
import jax.numpy as jnp
from jax import lax
from jax.sharding import PartitionSpec as P

STEPS = 8


def on_device(embeddings, best_start, bounds_start, proposals):
    row_count = embeddings.shape[0]
    prop_count = proposals.shape[1]
    own_index = lax.axis_index(("pts", "grp"))
    first_row = own_index * row_count
    point_total = row_count * lax.axis_size(("pts", "grp"))
    local_ids = first_row + jnp.arange(row_count, dtype=jnp.int32)
    best_sim = best_start
    bounds = bounds_start
    gain_rows = []
    cover_rows = []
    flat_chosen = proposals.reshape(-1)
    flat_offset = flat_chosen - first_row
    flat_owned = (flat_offset >= 0) & (flat_offset < row_count)
    all_rows = jnp.take(embeddings, jnp.clip(flat_offset, 0, row_count - 1), axis=0)
    all_masked = jnp.where(flat_owned[:, None], all_rows, jnp.zeros_like(all_rows)).astype(
        jnp.float32
    )
    fetched_all = lax.psum(all_masked, ("pts", "grp")).astype(jnp.bfloat16)
    similarity_all = lax.dot_general(
        embeddings, fetched_all, (((1,), (1,)), ((), ())), preferred_element_type=jnp.float32
    )
    for step_index in range(STEPS):
        chosen = proposals[step_index]
        similarity = similarity_all[:, step_index * prop_count : (step_index + 1) * prop_count]
        clipped = jnp.maximum(similarity - best_sim[:, None], 0.0)
        partial_sums = jnp.sum(clipped, axis=0)
        gain_values = lax.psum(partial_sums, ("pts", "grp")) / point_total
        weights = (gain_values + 0.01) / (jnp.sum(gain_values) + 0.01 * prop_count)
        mixed = jnp.dot(similarity, weights, precision=lax.Precision.HIGHEST)
        best_sim = jnp.maximum(best_sim, mixed)
        cover_rows.append(lax.psum(jnp.sum(best_sim), ("pts", "grp")) / point_total)
        matches = local_ids[:, None] == chosen[None, :]
        refreshed = jnp.max(jnp.where(matches, gain_values[None, :], -1.0), axis=1)
        bounds = jnp.where(jnp.any(matches, axis=1), refreshed, bounds)
        gain_rows.append(gain_values)
    return (jnp.stack(gain_rows), jnp.stack(cover_rows), best_sim, bounds)


def solution(mesh):
    placed = (P(("pts", "grp"), None), P(("pts", "grp")), P(("pts", "grp")), P())
    return jax.shard_map(
        on_device,
        mesh=mesh,
        in_specs=placed,
        out_specs=(P(), P(), P(("pts", "grp")), P(("pts", "grp"))),
        check_vma=False,
    )
```

profile of v0, /device:TPU:0, one launch (start us, length us, event | category | flops | bytes accessed | tf_op | source)
XLA Modules:
  0.0 473.4 jit_solution(3717555113697132605)
XLA Ops:
  0.6 0.7 subtract_clamp_fusion
  1.5 6.0 %gather_fusion = bf16[256,1024]{1,0:T(8,128)(2,1)S(1)} fusion(bf16[4096,1024]{1,0:T(8,128)(2,1)} %param.4, s32[1024]{0:T(1024)S(1)} %pad_clamp_fusion), kind=kCustom, calls=%fused_computation | custom fusion | bytes 1049600 | tf_op jit(solution)/shard_map/jit(_take)/gather | solution.py:23
  7.9 53.3 %all-reduce.2 = bf16[256,1024]{1,0:T(8,128)(2,1)S(1)} all-reduce(f32[256,1024]{1,0:T(8,128)S(1)} %select_convert_fusion), channel_id=1, replica_groups=mesh['pts'=8,'grp'=4] {'pts','grp'}, use_global_device_ids=true, to_apply=%region_0.1 | all-reduce | flops 262144 | bytes 1572864 | tf_op jit(solution)/shard_map/psum | solution.py:27
  61.2 7.7 %convolution_bitcast_fusion = f32[4096,256]{0,1:T(8,128)} fusion(bf16[4096,1024]{1,0:T(8,128)(2,1)} %param.4, bf16[256,1024]{1,0:T(8,128)(2,1)S(1)} %all-reduce.2), kind=kOutput, calls=%fused_computation.1 | convolution fusion | flops 2147483648 | bytes 13107200 | tf_op jit(solution)/shard_map/dot_general | solution.py:28
  68.9 1.2 maximum_reduce_fusion.7
  70.1 38.8 %psum.120 = f32[32]{0:T(128)S(1)} all-reduce(f32[32]{0:T(128)S(1)} %maximum_reduce_fusion.7), channel_id=1, replica_groups=mesh['pts'=8,'grp'=4] {'pts','grp'}, use_global_device_ids=true, to_apply=%region_2.3 | all-reduce | flops 32 | bytes 256 | tf_op jit(solution)/shard_map/psum | solution.py:36
  110.2 1.4 fusion.23
  112.2 1.2 maximum_reduce_fusion.6
  113.4 39.3 %psum.121 = f32[32]{0:T(128)S(1)} all-reduce(f32[32]{0:T(128)S(1)} %maximum_reduce_fusion.6), channel_id=1, replica_groups=mesh['pts'=8,'grp'=4] {'pts','grp'}, use_global_device_ids=true, to_apply=%region_5.6 | all-reduce | flops 32 | bytes 256 | tf_op jit(solution)/shard_map/psum | solution.py:36
  154.0 1.4 fusion.21
  156.0 1.2 maximum_reduce_fusion.5
  157.2 40.6 %psum.122 = f32[32]{0:T(128)S(1)} all-reduce(f32[32]{0:T(128)S(1)} %maximum_reduce_fusion.5), channel_id=1, replica_groups=mesh['pts'=8,'grp'=4] {'pts','grp'}, use_global_device_ids=true, to_apply=%region_8.9 | all-reduce | flops 32 | bytes 256 | tf_op jit(solution)/shard_map/psum | solution.py:36
  199.1 1.4 fusion.19
  201.1 1.2 maximum_reduce_fusion.4
  202.3 39.3 %psum.123 = f32[32]{0:T(128)S(1)} all-reduce(f32[32]{0:T(128)S(1)} %maximum_reduce_fusion.4), channel_id=1, replica_groups=mesh['pts'=8,'grp'=4] {'pts','grp'}, use_global_device_ids=true, to_apply=%region_11.12 | all-reduce | flops 32 | bytes 256 | tf_op jit(solution)/shard_map/psum | solution.py:36
  242.9 1.4 fusion.17
  245.0 1.2 maximum_reduce_fusion.3
  246.2 40.6 %psum.124 = f32[32]{0:T(128)S(1)} all-reduce(f32[32]{0:T(128)S(1)} %maximum_reduce_fusion.3), channel_id=1, replica_groups=mesh['pts'=8,'grp'=4] {'pts','grp'}, use_global_device_ids=true, to_apply=%region_14.15 | all-reduce | flops 32 | bytes 256 | tf_op jit(solution)/shard_map/psum | solution.py:36
  288.0 1.4 fusion.15
  290.1 1.2 maximum_reduce_fusion.2
  291.3 39.5 %psum.125 = f32[32]{0:T(128)S(1)} all-reduce(f32[32]{0:T(128)S(1)} %maximum_reduce_fusion.2), channel_id=1, replica_groups=mesh['pts'=8,'grp'=4] {'pts','grp'}, use_global_device_ids=true, to_apply=%region_17.18 | all-reduce | flops 32 | bytes 256 | tf_op jit(solution)/shard_map/psum | solution.py:36
  332.1 1.4 fusion.13
  334.1 1.2 maximum_reduce_fusion.1
  335.3 40.6 %psum.126 = f32[32]{0:T(128)S(1)} all-reduce(f32[32]{0:T(128)S(1)} %maximum_reduce_fusion.1), channel_id=1, replica_groups=mesh['pts'=8,'grp'=4] {'pts','grp'}, use_global_device_ids=true, to_apply=%region_20.21 | all-reduce | flops 32 | bytes 256 | tf_op jit(solution)/shard_map/psum | solution.py:36
  377.2 1.4 fusion.11
  379.2 1.2 maximum_reduce_fusion
  380.4 39.3 %psum.127 = f32[32]{0:T(128)S(1)} all-reduce(f32[32]{0:T(128)S(1)} %maximum_reduce_fusion), channel_id=1, replica_groups=mesh['pts'=8,'grp'=4] {'pts','grp'}, use_global_device_ids=true, to_apply=%region_23.24 | all-reduce | flops 32 | bytes 256 | tf_op jit(solution)/shard_map/psum | solution.py:36
  420.3 0.7 fusion.7
  421.1 0.9 compare_reduce_fusion
  423.3 1.4 fusion.9
  424.7 1.2 fusion.89
  425.9 41.2 %all-reduce = (f32[]{:T(128)}, f32[]{:T(128)}, f32[]{:T(128)}, f32[]{:T(128)}, f32[]{:T(128)}, /*index=5*/f32[]{:T(128)}, f32[]{:T(128)}, f32[]{:T(128)}) all-reduce(f32[]{:T(128)} %get-tuple-element.42, f32[]{:T(128)} %get-tuple-element.40, f32[]{:T(128)} %get-tuple-element.38, ...), channel_id=1, replica_groups=mesh['pts'=8,'grp'=4] {'pts','grp'}, use_global_device_ids=true, to_apply=%region_25.26 | all-reduce | flops 8 | bytes 64 | tf_op jit(solution)/shard_map/psum | solution.py:40
  (34 shorter events, 11.4 us)
Async XLA Ops:
  0.6 7.0 %copy-start.1 = (s32[8,32]{1,0:T(8,128)S(1)}, s32[8,32]{1,0:T(8,128)}, u32[]{:S(2)}) copy-start(s32[8,32]{1,0:T(8,128)} %param.7) | copy-start | bytes 3076
  61.2 7.7 %copy-start = (f32[4096]{0:T(1024)S(1)}, f32[4096]{0:T(1024)}, u32[]{:S(2)}) copy-start(f32[4096]{0:T(1024)} %param.5) | copy-start | bytes 49156
  70.1 351.9 %copy-start.2 = (f32[4096]{0:T(1024)S(1)}, f32[4096]{0:T(1024)}, u32[]{:S(2)}) copy-start(f32[4096]{0:T(1024)} %param.6) | copy-start | bytes 49156
where the time goes:
time: 475 us; the launch traced here: 473 us
  blocking collectives  413 us (87%)
  other arithmetic  23.2 us (5%)
  matrix products  19.1 us (4%)
  between operations  11.1 us (2%)
  local copies, waits for them, and re-layouts  7.49 us (2%)
    psum x8, blocking collectives, on_device(): gain_values = lax.psum(partial_sums, ('pts', 'grp')) / point_total  318 us
    psum x1, blocking collectives, on_device(): fetched_all = lax.psum(all_masked, ('pts', 'grp')).astype(jnp.bfloat16)  53.3 us
    psum x1, blocking collectives, on_device(): cover_rows.append(lax.psum(jnp.sum(best_sim), ('pts', 'grp')) / point_total)  41.2 us
    dot_general x8, matrix products, on_device(): mixed = jnp.dot(similarity, weights, precision=lax.Precision.HIGHEST)  11.4 us
    reduce_sum x8, other arithmetic, on_device(): partial_sums = jnp.sum(clipped, axis=0)  9.6 us

commit v1 on v0

--- a/solution.py
+++ b/solution.py
@@ -33,7 +33,7 @@
         similarity = similarity_all[:, step_index * prop_count : (step_index + 1) * prop_count]
         clipped = jnp.maximum(similarity - best_sim[:, None], 0.0)
         partial_sums = jnp.sum(clipped, axis=0)
-        gain_values = lax.psum(partial_sums, ("pts", "grp")) / point_total
+        gain_values = lax.psum(lax.psum(partial_sums, "grp"), "pts") / point_total
         weights = (gain_values + 0.01) / (jnp.sum(gain_values) + 0.01 * prop_count)
         mixed = jnp.dot(similarity, weights, precision=lax.Precision.HIGHEST)
         best_sim = jnp.maximum(best_sim, mixed)

time: 475 us -> 346 us (0.73)
  blocking collectives: 413 us -> 283 us
    psum x8 -> x16, blocking collectives: 318 us -> 191 us  [on_device(): gain_values = lax.psum(lax.psum(partial_sums, 'grp'), 'pts') / point_total]
where the time goes in v1:
time: 346 us; the launch traced here: 344 us
  blocking collectives  283 us (82%)
  other arithmetic  23.2 us (7%)
  matrix products  19.1 us (6%)
  between operations  11.1 us (3%)
  local copies, waits for them, and re-layouts  7.49 us (2%)
    psum x16, blocking collectives, on_device(): gain_values = lax.psum(lax.psum(partial_sums, 'grp'), 'pts') / point_total  191 us
    psum x1, blocking collectives, on_device(): fetched_all = lax.psum(all_masked, ('pts', 'grp')).astype(jnp.bfloat16)  53.3 us
    psum x1, blocking collectives, on_device(): cover_rows.append(lax.psum(jnp.sum(best_sim), ('pts', 'grp')) / point_total)  39.3 us
    dot_general x8, matrix products, on_device(): mixed = jnp.dot(similarity, weights, precision=lax.Precision.HIGHEST)  11.4 us
    reduce_sum x8, other arithmetic, on_device(): partial_sums = jnp.sum(clipped, axis=0)  9.6 us
    dot_general x1, matrix products, on_device(): lax.dot_general(embeddings, fetched_all, (((1,), (1,)), ((), ())), prefer...  7.68 us

profile of v1, /device:TPU:0, one launch (start us, length us, event | category | flops | bytes accessed | tf_op | source)
XLA Modules:
  0.0 344.2 jit_solution(18254805858355119353)
XLA Ops:
  1.5 6.0 %gather_fusion = bf16[256,1024]{1,0:T(8,128)(2,1)S(1)} fusion(bf16[4096,1024]{1,0:T(8,128)(2,1)} %param.4, s32[1024]{0:T(1024)S(1)} %pad_clamp_fusion), kind=kCustom, calls=%fused_computation | custom fusion | bytes 1049600 | tf_op jit(solution)/shard_map/jit(_take)/gather | solution.py:23
  7.9 53.3 %all-reduce.2 = bf16[256,1024]{1,0:T(8,128)(2,1)S(1)} all-reduce(f32[256,1024]{1,0:T(8,128)S(1)} %select_convert_fusion), channel_id=1, replica_groups=mesh['pts'=8,'grp'=4] {'pts','grp'}, use_global_device_ids=true, to_apply=%region_0.1 | all-reduce | flops 262144 | bytes 1572864 | tf_op jit(solution)/shard_map/psum | solution.py:27
  61.2 7.7 %convolution_bitcast_fusion = f32[4096,256]{0,1:T(8,128)} fusion(bf16[4096,1024]{1,0:T(8,128)(2,1)} %param.4, bf16[256,1024]{1,0:T(8,128)(2,1)S(1)} %all-reduce.2), kind=kOutput, calls=%fused_computation.1 | convolution fusion | flops 2147483648 | bytes 13107200 | tf_op jit(solution)/shard_map/dot_general | solution.py:28
  68.9 1.2 maximum_reduce_fusion.7
  70.1 5.9 %psum.176 = f32[32]{0:T(128)S(1)} all-reduce(f32[32]{0:T(128)S(1)} %maximum_reduce_fusion.7), channel_id=1, replica_groups=mesh['pts'=8,'grp'=4] {'grp'}, use_global_device_ids=true, to_apply=%region_2.3 | all-reduce | flops 32 | bytes 256 | tf_op jit(solution)/shard_map/psum | solution.py:36
  76.0 18.6 %psum.177 = f32[32]{0:T(128)S(1)} all-reduce(f32[32]{0:T(128)S(1)} %psum.176), channel_id=1, replica_groups=mesh['pts'=8,'grp'=4] {'pts'}, use_global_device_ids=true, to_apply=%region_3.4 | all-reduce | flops 32 | bytes 256 | tf_op jit(solution)/shard_map/psum | solution.py:36
  95.9 1.4 fusion.23
  97.9 1.2 maximum_reduce_fusion.6
  99.1 5.7 %psum.178 = f32[32]{0:T(128)S(1)} all-reduce(f32[32]{0:T(128)S(1)} %maximum_reduce_fusion.6), channel_id=1, replica_groups=mesh['pts'=8,'grp'=4] {'grp'}, use_global_device_ids=true, to_apply=%region_6.7 | all-reduce | flops 32 | bytes 256 | tf_op jit(solution)/shard_map/psum | solution.py:36
  104.8 17.7 %psum.179 = f32[32]{0:T(128)S(1)} all-reduce(f32[32]{0:T(128)S(1)} %psum.178), channel_id=1, replica_groups=mesh['pts'=8,'grp'=4] {'pts'}, use_global_device_ids=true, to_apply=%region_7.8 | all-reduce | flops 32 | bytes 256 | tf_op jit(solution)/shard_map/psum | solution.py:36
  123.7 1.4 fusion.21
  125.7 1.2 maximum_reduce_fusion.5
  126.9 5.7 %psum.180 = f32[32]{0:T(128)S(1)} all-reduce(f32[32]{0:T(128)S(1)} %maximum_reduce_fusion.5), channel_id=1, replica_groups=mesh['pts'=8,'grp'=4] {'grp'}, use_global_device_ids=true, to_apply=%region_10.11 | all-reduce | flops 32 | bytes 256 | tf_op jit(solution)/shard_map/psum | solution.py:36
  132.6 18.5 %psum.181 = f32[32]{0:T(128)S(1)} all-reduce(f32[32]{0:T(128)S(1)} %psum.180), channel_id=1, replica_groups=mesh['pts'=8,'grp'=4] {'pts'}, use_global_device_ids=true, to_apply=%region_11.12 | all-reduce | flops 32 | bytes 256 | tf_op jit(solution)/shard_map/psum | solution.py:36
  152.4 1.4 fusion.19
  155.7 5.7 %psum.182 = f32[32]{0:T(128)S(1)} all-reduce(f32[32]{0:T(128)S(1)} %maximum_reduce_fusion.4), channel_id=1, replica_groups=mesh['pts'=8,'grp'=4] {'grp'}, use_global_device_ids=true, to_apply=%region_14.15 | all-reduce | flops 32 | bytes 256 | tf_op jit(solution)/shard_map/psum | solution.py:36
  161.3 17.7 %psum.183 = f32[32]{0:T(128)S(1)} all-reduce(f32[32]{0:T(128)S(1)} %psum.182), channel_id=1, replica_groups=mesh['pts'=8,'grp'=4] {'pts'}, use_global_device_ids=true, to_apply=%region_15.16 | all-reduce | flops 32 | bytes 256 | tf_op jit(solution)/shard_map/psum | solution.py:36
  180.3 1.4 fusion.17
  183.5 5.7 %psum.184 = f32[32]{0:T(128)S(1)} all-reduce(f32[32]{0:T(128)S(1)} %maximum_reduce_fusion.3), channel_id=1, replica_groups=mesh['pts'=8,'grp'=4] {'grp'}, use_global_device_ids=true, to_apply=%region_18.19 | all-reduce | flops 32 | bytes 256 | tf_op jit(solution)/shard_map/psum | solution.py:36
  189.2 18.5 %psum.185 = f32[32]{0:T(128)S(1)} all-reduce(f32[32]{0:T(128)S(1)} %psum.184), channel_id=1, replica_groups=mesh['pts'=8,'grp'=4] {'pts'}, use_global_device_ids=true, to_apply=%region_19.20 | all-reduce | flops 32 | bytes 256 | tf_op jit(solution)/shard_map/psum | solution.py:36
  209.0 1.4 fusion.15
  212.3 5.7 %psum.186 = f32[32]{0:T(128)S(1)} all-reduce(f32[32]{0:T(128)S(1)} %maximum_reduce_fusion.2), channel_id=1, replica_groups=mesh['pts'=8,'grp'=4] {'grp'}, use_global_device_ids=true, to_apply=%region_22.23 | all-reduce | flops 32 | bytes 256 | tf_op jit(solution)/shard_map/psum | solution.py:36
  218.0 17.6 %psum.187 = f32[32]{0:T(128)S(1)} all-reduce(f32[32]{0:T(128)S(1)} %psum.186), channel_id=1, replica_groups=mesh['pts'=8,'grp'=4] {'pts'}, use_global_device_ids=true, to_apply=%region_23.24 | all-reduce | flops 32 | bytes 256 | tf_op jit(solution)/shard_map/psum | solution.py:36
  236.9 1.4 fusion.13
  240.1 5.7 %psum.188 = f32[32]{0:T(128)S(1)} all-reduce(f32[32]{0:T(128)S(1)} %maximum_reduce_fusion.1), channel_id=1, replica_groups=mesh['pts'=8,'grp'=4] {'grp'}, use_global_device_ids=true, to_apply=%region_26.27 | all-reduce | flops 32 | bytes 256 | tf_op jit(solution)/shard_map/psum | solution.py:36
  245.8 18.7 %psum.189 = f32[32]{0:T(128)S(1)} all-reduce(f32[32]{0:T(128)S(1)} %psum.188), channel_id=1, replica_groups=mesh['pts'=8,'grp'=4] {'pts'}, use_global_device_ids=true, to_apply=%region_27.28 | all-reduce | flops 32 | bytes 256 | tf_op jit(solution)/shard_map/psum | solution.py:36
  265.8 1.4 fusion.11
  269.0 5.8 %psum.190 = f32[32]{0:T(128)S(1)} all-reduce(f32[32]{0:T(128)S(1)} %maximum_reduce_fusion), channel_id=1, replica_groups=mesh['pts'=8,'grp'=4] {'grp'}, use_global_device_ids=true, to_apply=%region_30.31 | all-reduce | flops 32 | bytes 256 | tf_op jit(solution)/shard_map/psum | solution.py:36
  274.8 17.6 %psum.191 = f32[32]{0:T(128)S(1)} all-reduce(f32[32]{0:T(128)S(1)} %psum.190), channel_id=1, replica_groups=mesh['pts'=8,'grp'=4] {'pts'}, use_global_device_ids=true, to_apply=%region_31.32 | all-reduce | flops 32 | bytes 256 | tf_op jit(solution)/shard_map/psum | solution.py:36
  295.9 1.4 fusion.9
  297.4 1.2 fusion.89
  298.6 39.3 %all-reduce = (f32[]{:T(128)}, f32[]{:T(128)}, f32[]{:T(128)}, f32[]{:T(128)}, f32[]{:T(128)}, /*index=5*/f32[]{:T(128)}, f32[]{:T(128)}, f32[]{:T(128)}) all-reduce(f32[]{:T(128)} %get-tuple-element.42, f32[]{:T(128)} %get-tuple-element.40, f32[]{:T(128)} %get-tuple-element.38, ...), channel_id=1, replica_groups=mesh['pts'=8,'grp'=4] {'pts','grp'}, use_global_device_ids=true, to_apply=%region_33.34 | all-reduce | flops 8 | bytes 64 | tf_op jit(solution)/shard_map/psum | solution.py:40
  (42 shorter events, 19.9 us)
Async XLA Ops:
  0.6 7.0 %copy-start.1 = (s32[8,32]{1,0:T(8,128)S(1)}, s32[8,32]{1,0:T(8,128)}, u32[]{:S(2)}) copy-start(s32[8,32]{1,0:T(8,128)} %param.7) | copy-start | bytes 3076
  61.2 7.7 %copy-start = (f32[4096]{0:T(1024)S(1)}, f32[4096]{0:T(1024)}, u32[]{:S(2)}) copy-start(f32[4096]{0:T(1024)} %param.5) | copy-start | bytes 49156
  70.1 224.6 %copy-start.2 = (f32[4096]{0:T(1024)S(1)}, f32[4096]{0:T(1024)}, u32[]{:S(2)}) copy-start(f32[4096]{0:T(1024)} %param.6) | copy-start | bytes 49156

commit v2 on v0

--- a/solution.py
+++ b/solution.py
@@ -33,7 +33,7 @@
         similarity = similarity_all[:, step_index * prop_count : (step_index + 1) * prop_count]
         clipped = jnp.maximum(similarity - best_sim[:, None], 0.0)
         partial_sums = jnp.sum(clipped, axis=0)
-        gain_values = lax.psum(partial_sums, ("pts", "grp")) / point_total
+        gain_values = jnp.sum(lax.all_gather(partial_sums, ("pts", "grp")), axis=0) / point_total
         weights = (gain_values + 0.01) / (jnp.sum(gain_values) + 0.01 * prop_count)
         mixed = jnp.dot(similarity, weights, precision=lax.Precision.HIGHEST)
         best_sim = jnp.maximum(best_sim, mixed)

time: 475 us -> 492 us (1.036)
  local copies, waits for them, and re-layouts: 7.49 us -> 24.5 us
    unnamed x0 -> x8, blocking collectives: none -> 320 us
    psum x8 -> x0, blocking collectives: 318 us -> none  [on_device(): gain_values = lax.psum(partial_sums, ('pts', 'grp')) / point_total]
    unnamed x6 -> x26, local copies, waits for them, and re-layouts: 0.01 us -> 16.5 us
where the time goes in v2:
time: 492 us; the launch traced here: 490 us
  blocking collectives  414 us (84%)
  local copies, waits for them, and re-layouts  24.5 us (5%)
  other arithmetic  22.4 us (5%)
  matrix products  17.2 us (3%)
  between operations  11.1 us (2%)
    unnamed x8, blocking collectives  320 us
    psum x1, blocking collectives, on_device(): fetched_all = lax.psum(all_masked, ('pts', 'grp')).astype(jnp.bfloat16)  53.3 us
    psum x1, blocking collectives, on_device(): cover_rows.append(lax.psum(jnp.sum(best_sim), ('pts', 'grp')) / point_total)  41.2 us
    unnamed x26, local copies, waits for them, and re-layouts  16.5 us
    dot_general x8, matrix products, on_device(): mixed = jnp.dot(similarity, weights, precision=lax.Precision.HIGHEST)  11.5 us

profile of v2, /device:TPU:0, one launch (start us, length us, event | category | flops | bytes accessed | tf_op | source)
XLA Modules:
  0.0 489.6 jit_solution(15097443998387821426)
XLA Ops:
  1.5 6.0 %gather_fusion = bf16[256,1024]{1,0:T(8,128)(2,1)S(1)} fusion(bf16[4096,1024]{1,0:T(8,128)(2,1)} %param.4, s32[1024]{0:T(1024)S(1)} %pad_clamp_fusion), kind=kCustom, calls=%fused_computation | custom fusion | bytes 1049600 | tf_op jit(solution)/shard_map/jit(_take)/gather | solution.py:23
  7.9 53.3 %all-reduce.10 = bf16[256,1024]{1,0:T(8,128)(2,1)S(1)} all-reduce(f32[256,1024]{1,0:T(8,128)S(1)} %select_convert_fusion), channel_id=1, replica_groups=mesh['pts'=8,'grp'=4] {'pts','grp'}, use_global_device_ids=true, to_apply=%region_0.1 | all-reduce | flops 262144 | bytes 1572864 | tf_op jit(solution)/shard_map/psum | solution.py:27
  61.2 5.8 %convolution_bitcast_fusion = f32[4096,256]{0,1:T(8,128)S(1)} fusion(bf16[4096,1024]{1,0:T(8,128)(2,1)} %param.4, bf16[256,1024]{1,0:T(8,128)(2,1)S(1)} %all-reduce.10), kind=kOutput, calls=%fused_computation.1 | convolution fusion | flops 2147483648 | bytes 13107200 | tf_op jit(solution)/shard_map/dot_general | solution.py:28
  67.0 1.9 copy-done
  69.9 39.0 %all-reduce = f32[1024]{0:T(1024)S(1)} all-reduce(f32[1024]{0:T(1024)} %copy-done.4), channel_id=2, replica_groups=mesh['pts'=8,'grp'=4] {'pts','grp'}, use_global_device_ids=true, to_apply=%add | all-reduce | flops 1024 | bytes 8192
  110.3 1.4 fusion.23
  112.4 1.2 maximum_reduce_fusion.6
  114.2 1.4 dynamic-update-slice.1
  115.5 39.5 %all-reduce.1 = f32[1024]{0:T(1024)S(1)} all-reduce(f32[1024]{0:T(1024)} %dynamic-update-slice.1), channel_id=3, replica_groups=mesh['pts'=8,'grp'=4] {'pts','grp'}, use_global_device_ids=true, to_apply=%add.1 | all-reduce | flops 1024 | bytes 8192
  156.4 1.4 fusion.21
  158.5 1.2 maximum_reduce_fusion.5
  160.3 1.4 dynamic-update-slice.2
  161.6 40.8 %all-reduce.2 = f32[1024]{0:T(1024)S(1)} all-reduce(f32[1024]{0:T(1024)} %dynamic-update-slice.2), channel_id=4, replica_groups=mesh['pts'=8,'grp'=4] {'pts','grp'}, use_global_device_ids=true, to_apply=%add.2 | all-reduce | flops 1024 | bytes 8192
  203.8 1.4 fusion.19
  205.9 1.2 maximum_reduce_fusion.4
  207.7 1.4 dynamic-update-slice.3
  209.0 39.5 %all-reduce.3 = f32[1024]{0:T(1024)S(1)} all-reduce(f32[1024]{0:T(1024)} %dynamic-update-slice.3), channel_id=5, replica_groups=mesh['pts'=8,'grp'=4] {'pts','grp'}, use_global_device_ids=true, to_apply=%add.3 | all-reduce | flops 1024 | bytes 8192
  249.9 1.4 fusion.17
  253.8 1.4 dynamic-update-slice.4
  255.2 41.0 %all-reduce.4 = f32[1024]{0:T(1024)S(1)} all-reduce(f32[1024]{0:T(1024)} %dynamic-update-slice.4), channel_id=6, replica_groups=mesh['pts'=8,'grp'=4] {'pts','grp'}, use_global_device_ids=true, to_apply=%add.4 | all-reduce | flops 1024 | bytes 8192
  297.6 1.4 fusion.15
  301.4 1.4 dynamic-update-slice.5
  302.7 39.5 %all-reduce.5 = f32[1024]{0:T(1024)S(1)} all-reduce(f32[1024]{0:T(1024)} %dynamic-update-slice.5), channel_id=7, replica_groups=mesh['pts'=8,'grp'=4] {'pts','grp'}, use_global_device_ids=true, to_apply=%add.5 | all-reduce | flops 1024 | bytes 8192
  343.6 1.4 fusion.13
  347.5 1.4 dynamic-update-slice.6
  348.8 40.8 %all-reduce.6 = f32[1024]{0:T(1024)S(1)} all-reduce(f32[1024]{0:T(1024)} %dynamic-update-slice.6), channel_id=8, replica_groups=mesh['pts'=8,'grp'=4] {'pts','grp'}, use_global_device_ids=true, to_apply=%add.6 | all-reduce | flops 1024 | bytes 8192
  391.0 1.4 fusion.11
  394.9 1.4 dynamic-update-slice.7
  396.3 39.5 %all-reduce.7 = f32[1024]{0:T(1024)S(1)} all-reduce(f32[1024]{0:T(1024)} %dynamic-update-slice.7), channel_id=9, replica_groups=mesh['pts'=8,'grp'=4] {'pts','grp'}, use_global_device_ids=true, to_apply=%add.7 | all-reduce | flops 1024 | bytes 8192
  439.5 1.4 fusion.9
  440.9 1.2 fusion.89
  442.1 41.2 %all-reduce.8 = (f32[]{:T(128)}, f32[]{:T(128)}, f32[]{:T(128)}, f32[]{:T(128)}, f32[]{:T(128)}, /*index=5*/f32[]{:T(128)}, f32[]{:T(128)}, f32[]{:T(128)}) all-reduce(f32[]{:T(128)} %get-tuple-element.42, f32[]{:T(128)} %get-tuple-element.40, f32[]{:T(128)} %get-tuple-element.38, ...), channel_id=1, replica_groups=mesh['pts'=8,'grp'=4] {'pts','grp'}, use_global_device_ids=true, to_apply=%region_25.26 | all-reduce | flops 8 | bytes 64 | tf_op jit(solution)/shard_map/psum | solution.py:40
  (70 shorter events, 24.7 us)
Async XLA Ops:
  0.6 7.0 %copy-start.2 = (s32[8,32]{1,0:T(8,128)S(1)}, s32[8,32]{1,0:T(8,128)}, u32[]{:S(2)}) copy-start(s32[8,32]{1,0:T(8,128)} %param.7) | copy-start | bytes 3076
  61.2 7.7 %copy-start.1 = (f32[4096]{0:T(1024)S(1)}, f32[4096]{0:T(1024)}, u32[]{:S(2)}) copy-start(f32[4096]{0:T(1024)} %param.5) | copy-start | bytes 49156
  67.0 1.9 copy-start
  69.3 0.6 copy-start.4
  110.3 327.9 %copy-start.3 = (f32[4096]{0:T(1024)S(1)}, f32[4096]{0:T(1024)}, u32[]{:S(2)}) copy-start(f32[4096]{0:T(1024)} %param.6) | copy-start | bytes 49156
